TPU v7x, 256 devices: a whole 4x4x8 slice. The times are simulated.
256 devices in a mesh: dap: 16 (over x, z_lo), cplx: 16 (over y, z_hi, core).
Axes of the slice: x: 4, y: 4, z: 8 (z_hi: 2, z_lo: 4; z = z_hi * 4 + z_lo), core: 2. Of those that a mesh axis runs over, the one named last changes fastest.
Arguments:
- pair: bfloat16 [192, 3072, 128], P('dap', 'cplx'), parts along dimension 1, may hold values from -6 to 6
- cotangent: bfloat16 [192, 3072, 128], P('dap', 'cplx'), parts along dimension 1, may hold values from -6 to 6
- residue_mask: int32 [3072], P('cplx'), parts along dimension 0, may hold values 0 or 1
- chain_ids: int32 [3072], P('cplx'), parts along dimension 0, may hold values from 0 to 2, never falling along the last dimension, each value on 1 to 96 neighbouring positions
- chain_embed: float32 [2, 128], replicated, may hold values from -4 to 4
- out_norm_gain: float32 [128], replicated, may hold values from 0.25 to 1.75
- out_proj: bfloat16 [128, 512], replicated, may hold values from -0.5 to 0.5
- out_gate: bfloat16 [128, 128], replicated, may hold values from -0.5 to 0.5
- out_mid_gain: float32 [128], replicated, may hold values from 0.25 to 1.75
- out_final: bfloat16 [128, 128], replicated, may hold values from -0.5 to 0.5
- in_norm_gain: float32 [128], replicated, may hold values from 0.25 to 1.75
- in_proj: bfloat16 [128, 512], replicated, may hold values from -0.5 to 0.5
- in_gate: bfloat16 [128, 128], replicated, may hold values from -0.5 to 0.5
- in_mid_gain: float32 [128], replicated, may hold values from 0.25 to 1.75
- in_final: bfloat16 [128, 128], replicated, may hold values from -0.5 to 0.5
Outputs:
- pair_grad: bfloat16 [192, 3072, 128], P('dap', 'cplx'), parts along dimension 1
- grad_proj: float32 [2048, 512], P('cplx'), parts along dimension 0
- grad_gate: float32 [2048, 128], P('cplx'), parts along dimension 0
- grad_final: float32 [2048, 128], P('cplx'), parts along dimension 0
- grad_norm_gain: float32 [2048], P('cplx'), parts along dimension 0
- grad_mid_gain: float32 [2048], P('cplx'), parts along dimension 0
There are 16 independent parts, one for each index of `cplx`. A program takes and returns all parts, laid end to end along the dimension named above; an argument that names none is the same for every part. Nothing has to cross between parts.
Inputs may be any that keep to these rules, and one draw needn't show every extreme that they name: `chain_ids`: chain numbers never fall along the residues; each chain has at most 96 residues.
All inputs are finite; a program needn't handle non-finite values.
Results may differ from a plain program's by a relative error of at most 0.019.
Values may be sent and summed in bfloat16 or wider, within the bound.
No kernel may reach another device: no remote copies, remote signals or barrier semaphores. Data moves between devices by JAX's collectives and lax.ppermute only.
A program may use at most 128 MiB of HBM per device.

v0:
```python
import jax
import jax.numpy as jnp
from jax import lax
from jax.sharding import PartitionSpec as P


def together(arrays, axis):
    ends = [0]
    for a in arrays:
        ends.append(ends[-1] + a.size)
    subtotal = lax.psum(jnp.concatenate([a.ravel() for a in arrays]), axis)
    return tuple((subtotal[b:e].reshape(a.shape) for a, b, e in zip(arrays, ends, ends[1:])))


def layer_norm(values_in, gain):
    average = jnp.mean(values_in, axis=-1, keepdims=True)
    centred = values_in - average
    variance = jnp.mean(centred * centred, axis=-1, keepdims=True)
    return centred * lax.rsqrt(variance + 1e-05) * gain


def gated_pair(projected, pair_mask, hidden_width):
    masked = pair_mask[..., None]
    left_act = (
        masked
        * jax.nn.sigmoid(projected[..., :hidden_width])
        * projected[..., hidden_width : 2 * hidden_width]
    )
    right_act = (
        masked
        * jax.nn.sigmoid(projected[..., 2 * hidden_width : 3 * hidden_width])
        * projected[..., 3 * hidden_width :]
    )
    return (left_act, right_act)


def shards(
    pair,
    cotangent,
    residue_mask,
    chain_ids,
    chain_embed,
    out_norm_gain,
    out_proj,
    out_gate,
    out_mid_gain,
    out_final,
    in_norm_gain,
    in_proj,
    in_gate,
    in_mid_gain,
    in_final,
):
    f32 = jnp.float32
    bf16 = jnp.bfloat16
    row_count = pair.shape[0]
    res_count = pair.shape[1]
    hidden_width = out_final.shape[0]
    inv_count = 1.0 / res_count
    row_start = lax.axis_index("dap") * row_count
    row_mask = lax.dynamic_slice_in_dim(residue_mask, row_start, row_count, 0)
    row_chain = lax.dynamic_slice_in_dim(chain_ids, row_start, row_count, 0)
    pair_mask = (row_mask[:, None] * residue_mask[None, :]).astype(f32)
    same_chain = row_chain[:, None] == chain_ids[None, :]
    start = pair.astype(f32) + jnp.where(same_chain[..., None], chain_embed[1], chain_embed[0])
    out_normed = layer_norm(start, out_norm_gain).astype(bf16)
    projected = jnp.dot(out_normed, out_proj, preferred_element_type=f32)
    left_act, right_act = gated_pair(projected, pair_mask, hidden_width)
    left_b = left_act.astype(bf16)
    right_b = right_act.astype(bf16)
    x_out = jnp.einsum(
        "ikc,jkc->ijc",
        left_b,
        lax.all_gather(right_b, "dap", axis=0, tiled=True),
        preferred_element_type=f32,
    )
    y_out = layer_norm(x_out, out_mid_gain).astype(bf16)
    update = jax.nn.sigmoid(jnp.dot(out_normed, out_gate, preferred_element_type=f32)) * jnp.dot(
        y_out, out_final, preferred_element_type=f32
    )
    pair_mid = (start + update).astype(bf16)
    mid_f32 = pair_mid.astype(f32)
    normed_f32, norm_back = jax.vjp(layer_norm, mid_f32, in_norm_gain)
    in_normed = normed_f32.astype(bf16)
    proj_in = jnp.dot(in_normed, in_proj, preferred_element_type=f32)
    (left_in, right_in), glu_back = jax.vjp(
        lambda proj_val: gated_pair(proj_val, pair_mask, hidden_width), proj_in
    )
    left_ib = left_in.astype(bf16)
    right_ib = right_in.astype(bf16)
    columns = lax.all_to_all(left_ib, "dap", split_axis=1, concat_axis=0, tiled=True)
    left_block = columns
    x_in = jnp.einsum(
        "kic,kjc->ijc",
        left_block,
        lax.all_gather(right_ib, "dap", axis=0, tiled=True),
        preferred_element_type=f32,
    )
    y_f32, mid_back = jax.vjp(layer_norm, x_in, in_mid_gain)
    y_in = y_f32.astype(bf16)
    logit = jnp.dot(in_normed, in_gate, preferred_element_type=f32)
    value = jnp.dot(y_in, in_final, preferred_element_type=f32)
    sigma = jax.nn.sigmoid(logit)
    upstream = cotangent.astype(f32)
    grad_value = (upstream * sigma).astype(bf16)
    grad_logit = (upstream * value * sigma * (1.0 - sigma)).astype(bf16)
    grad_final = jnp.einsum("ijc,ijd->cd", y_in, grad_value, preferred_element_type=f32) * inv_count
    grad_gate = (
        jnp.einsum("ijc,ijd->cd", in_normed, grad_logit, preferred_element_type=f32) * inv_count
    )
    grad_y = jnp.dot(grad_value, in_final.T, preferred_element_type=f32)
    grad_x, grad_mid = mid_back(grad_y)
    grad_x_b = grad_x.astype(bf16)
    shard_rows = lax.all_gather(grad_x_b, "dap", axis=0, tiled=True)
    left_block = left_ib
    grad_right = jnp.einsum("kic,ijc->kjc", left_block, shard_rows, preferred_element_type=f32)
    new_block = jnp.einsum("kjc,ijc->kic", right_ib, shard_rows, preferred_element_type=f32)
    grad_p = glu_back((new_block, grad_right))[0].astype(bf16)
    grad_proj = jnp.einsum("ijc,ijd->cd", in_normed, grad_p, preferred_element_type=f32) * inv_count
    grad_normed = jnp.dot(grad_p, in_proj.T, preferred_element_type=f32) + jnp.dot(
        grad_logit, in_gate.T, preferred_element_type=f32
    )
    grad_z, grad_norm = norm_back(grad_normed)
    pair_grad = (upstream + grad_z).astype(bf16)
    reduced = tuple(
        (
            part.astype(jnp.float32)
            for part in together(
                (
                    grad_proj.astype(jnp.bfloat16),
                    grad_gate.astype(jnp.bfloat16),
                    grad_final.astype(jnp.bfloat16),
                    (grad_norm * inv_count).astype(jnp.bfloat16),
                    (grad_mid * inv_count).astype(jnp.bfloat16),
                ),
                "dap",
            )
        )
    )
    return (pair_grad, reduced[0], reduced[1], reduced[2], reduced[3], reduced[4])


def solution(mesh):
    placed = (
        P("dap", "cplx", None),
        P("dap", "cplx", None),
        P("cplx"),
        P("cplx"),
        P(),
        P(),
        P(),
        P(),
        P(),
        P(),
        P(),
        P(),
        P(),
        P(),
        P(),
    )
    return jax.shard_map(
        shards,
        mesh=mesh,
        in_specs=placed,
        out_specs=(
            P("dap", "cplx", None),
            P("cplx", None),
            P("cplx", None),
            P("cplx", None),
            P("cplx"),
            P("cplx"),
        ),
        check_vma=False,
    )
```

profile of v0, /device:TPU:8, one launch (start us, length us, event | category | flops | bytes accessed | tf_op | source)
XLA Modules:
  0.0 931.0 jit_solution(3358620269729586650)
XLA Ops:
  11.6 2.3 multiply_reduce_fusion.4
  18.7 2.8 fusion.12
  21.5 204.8 %all-gather.4.cloned.1.call-done = bf16[192,192,128]{2,1,0:T(8,128)(2,1)} async-done(((bf16[12,192,128]{2,1,0:T(8,128)(2,1)}), bf16[192,192,128]{2,1,0:T(8,128)(2,1)}) %all-gather.4.cloned.1.call-update) | async-done | bytes 9437200 | tf_op jit(solution)/shard_map/all_gather | solution.py:74
  226.2 17.4 %copy.46 = bf16[192,192,128]{1,0,2:T(8,128)(2,1)} copy(bf16[192,192,128]{2,1,0:T(8,128)(2,1)} %all-gather.4.cloned.1.call-done) | data formatting | bytes 18874368 | tf_op jit(solution)/shard_map/all_gather | solution.py:74
  243.6 8.2 bitcast_reduce_fusion
  260.7 4.3 all-to-all-start
  266.1 41.9 %all-to-all-done = bf16[12,192,128]{2,0,1:T(8,128)(2,1)} async-done(((bf16[12,192,128]{2,0,1:T(8,128)(2,1)}), bf16[12,192,128]{2,0,1:T(8,128)(2,1)}, u32[]{:S(2)}, u32[]{:S(2)}) %all-to-all-start) | async-done | bytes 589856 | tf_op jit(solution)/shard_map/all_to_all | solution.py:91
  312.1 163.0 %all-gather.6.cloned.1.call-done = bf16[192,192,128]{2,1,0:T(8,128)(2,1)} async-done(((bf16[12,192,128]{2,1,0:T(8,128)(2,1)}), bf16[192,192,128]{2,1,0:T(8,128)(2,1)}) %all-gather.6.cloned.1.call-update) | async-done | bytes 9437200 | tf_op jit(solution)/shard_map/all_gather | solution.py:96
  475.0 17.4 %copy.52 = bf16[192,192,128]{1,0,2:T(8,128)(2,1)} copy(bf16[192,192,128]{2,1,0:T(8,128)(2,1)} %all-gather.6.cloned.1.call-done) | data formatting | bytes 18874368 | tf_op jit(solution)/shard_map/all_gather | solution.py:96
  492.4 7.6 fusion.82
  500.1 2.2 copy.54
  506.4 2.3 add_convert_fusion.1
  509.1 2.6 copy.59
  511.7 2.6 copy.56
  514.3 2.7 fusion.15
  517.0 198.6 %all-gather.8.cloned.1.call-done = bf16[192,192,128]{2,1,0:T(8,128)(2,1)} async-done(((bf16[12,192,128]{2,1,0:T(8,128)(2,1)}), bf16[192,192,128]{2,1,0:T(8,128)(2,1)}) %all-gather.8.cloned.1.call-update) | async-done | bytes 9437200 | tf_op jit(solution)/shard_map/all_gather | solution.py:114
  715.6 17.4 %copy.55 = bf16[192,192,128]{1,0,2:T(8,128)(2,1)} copy(bf16[192,192,128]{2,1,0:T(8,128)(2,1)} %all-gather.8.cloned.1.call-done) | data formatting | bytes 18874368 | tf_op jit(solution)/shard_map/all_gather | solution.py:114
  733.0 9.5 %fusion.84 = f32[128,192,12]{1,2,0:T(8,128)} fusion(bf16[192,192,128]{1,0,2:T(8,128)(2,1)} %copy.55, bf16[12,192,128]{1,0,2:T(8,128)(2,1)} %copy.59), kind=kOutput, calls=%fused_computation.145 | convolution fusion | flops 113246208 | bytes 11206656 | tf_op jit(solution)/shard_map/kjc,ijc->kic/dot_general | solution.py:117
  742.5 2.7 copy.60
  745.2 7.9 fusion.83
  753.1 2.7 copy.57
  755.8 3.7 bitcast_multiply_fusion.3
  767.7 2.5 fusion.22
  770.2 149.9 %all-reduce.6.cloned.1.call-done = bf16[98560]{0:T(1024)(128)(2,1)} async-done(((bf16[98560]{0:T(1024)(128)(2,1)}), bf16[98560]{0:T(1024)(128)(2,1)}) %all-reduce.6.cloned.1.call-update) | async-done | bytes 197136 | tf_op jit(solution)/shard_map/psum | solution.py:11
  (98 shorter events, 39.8 us)
Async XLA Ops:
  7.2 249.1 %copy-start = (bf16[128,512]{1,0:T(8,128)(2,1)S(1)}, bf16[128,512]{1,0:T(8,128)(2,1)}, u32[]{:S(2)}) copy-start(bf16[128,512]{1,0:T(8,128)(2,1)} %param.26) | copy-start | bytes 393220
  7.2 6.9 copy-start.5
  7.2 6.7 copy-start.16
  7.2 6.8 copy-start.18
  7.2 6.8 copy-start.11
  7.2 219.0 %all-gather.4.cloned.1.call-start = ((), (), s32[]{:S(2)}) async-start(), calls=%async_computation.1 | async-start | bytes 10027008 | tf_op jit(solution)/shard_map/all_gather | solution.py:74
  16.7 2.0 copy-start.19
  16.7 458.3 %all-gather.6.cloned.1.call-start = ((), (), s32[]{:S(2)}) async-start(), calls=%async_computation.2 | async-start | bytes 10027008 | tf_op jit(solution)/shard_map/all_gather | solution.py:96
  251.8 0.7 copy-start.17
  252.5 1.3 copy-start.8
  252.5 1.3 copy-start.12
  253.8 2.5 copy-start.15
  257.1 2.3 copy-start.1
  259.4 1.3 copy-start.6
  259.4 5.8 copy-start.13
  260.7 47.2 %all-to-all-start = ((bf16[12,192,128]{2,0,1:T(8,128)(2,1)}), bf16[12,192,128]{2,0,1:T(8,128)(2,1)}, u32[]{:S(2)}, u32[]{:S(2)}) async-start(bf16[12,192,128]{2,0,1:T(8,128)(2,1)} %copy.49), calls=%async_computation | async-start | bytes 1572864 | tf_op jit(solution)/shard_map/all_to_all | solution.py:91
  265.0 450.6 %all-gather.8.cloned.1.call-start = ((), (), s32[]{:S(2)}) async-start(), calls=%async_computation.3 | async-start | bytes 10027008 | tf_op jit(solution)/shard_map/all_gather | solution.py:114
  502.3 1.1 copy-start.2
  502.3 1.1 copy-start.10
  502.3 1.0 copy-start.14
  508.8 411.3 %all-reduce.6.cloned.1.call-start = ((), (), s32[]{:S(2)}) async-start(), calls=%async_computation.4 | async-start | bytes 397312 | tf_op jit(solution)/shard_map/psum | solution.py:11
  760.8 1.1 copy-start.7
  761.6 1.2 copy-start.3
  764.8 2.9 copy-start.4
  (1 other events, 0.7 us)
Sparse Core Ops, SparseCore 0:
  16.8 209.3 all-gather.3
  259.5 215.4 all-gather.5
  508.9 206.6 all-gather.7
  767.8 152.2 all-reduce.5
where the time goes:
time: 933 us; the launch traced here: 931 us
  waiting for transfers between devices  758 us (81%)
  local copies, waits for them, and re-layouts  78.5 us (8%)
  matrix products  49.2 us (5%)
  other arithmetic  26.1 us (3%)
  between operations  14.2 us (2%)
    all_gather x1, waiting for transfers between devices, shards(): lax.all_gather(right_b, 'dap', axis=0, tiled=True)  205 us
    all_gather x1, waiting for transfers between devices, shards(): shard_rows = lax.all_gather(grad_x_b, 'dap', axis=0, tiled=True)  199 us
    all_gather x1, waiting for transfers between devices, shards(): lax.all_gather(right_ib, 'dap', axis=0, tiled=True)  163 us
    psum x1, waiting for transfers between devices, together(): subtotal = lax.psum(jnp.concatenate([a.ravel() for a in arrays]), axis)  150 us
    all_to_all x1, waiting for transfers between devices, shards(): lax.all_to_all(left_ib, 'dap', split_axis=1, concat_axis=0, tiled=True)  41.9 us
  transfers between devices with their start and end apart: 5, of which 5 were waited for; matrix products, arithmetic and copies ran while one was open for 2% of the time, Pallas kernels for 0%

commit v1 on v0

--- a/solution.py
+++ b/solution.py
@@ -93,7 +93,9 @@
     x_in = jnp.einsum(
         "kic,kjc->ijc",
         left_block,
-        lax.all_gather(right_ib, "dap", axis=0, tiled=True),
+        jnp.concatenate(
+            lax.all_to_all(jnp.stack([right_ib] * lax.axis_size("dap")), "dap", 0, 0), axis=0
+        ),
         preferred_element_type=f32,
     )
     y_f32, mid_back = jax.vjp(layer_norm, x_in, in_mid_gain)

time: 933 us -> 961 us (1.030)
  blocking collectives: 0 us -> 25.5 us
    all_gather x1 -> x0, waiting for transfers between devices: 163 us -> none  [shards(): lax.all_gather(right_ib, 'dap', axis=0, tiled=True)]
    all_to_all x1, waiting for transfers between devices: 41.9 us -> 202 us  [shards(): lax.all_to_all(jnp.stack([right_ib] * lax.axis_size('dap')), 'dap', 0, 0)]
    all_to_all x0 -> x1, blocking collectives: none -> 25.5 us  [shards(): lax.all_to_all(left_ib, 'dap', split_axis=1, concat_axis=0, tiled=True)]
    all_gather x1 -> x0, local copies, waits for them, and re-layouts: 17.4 us -> none  [shards(): lax.all_gather(right_ib, 'dap', axis=0, tiled=True)]
    reshape x0 -> x1, local copies, waits for them, and re-layouts: none -> 17.4 us  [shards(): jnp.concatenate(lax.all_to_all(jnp.stack([right_ib] * lax.axis_size('dap'...]
  transfers between devices with their start and end apart: 5 -> 4, of which waited for: 5 -> 4; matrix products, arithmetic and copies ran while one was open for 2% -> 2% of each run, Pallas kernels for 0% -> 0%
where the time goes in v1:
time: 961 us; the launch traced here: 960 us
  waiting for transfers between devices  755 us (79%)
  local copies, waits for them, and re-layouts  85.4 us (9%)
  matrix products  49.3 us (5%)
  blocking collectives  25.5 us (3%)
  other arithmetic  24.9 us (3%)
  between operations  14.2 us (1%)
    all_gather x1, waiting for transfers between devices, shards(): lax.all_gather(right_b, 'dap', axis=0, tiled=True)  205 us
    all_to_all x1, waiting for transfers between devices, shards(): lax.all_to_all(jnp.stack([right_ib] * lax.axis_size('dap')), 'dap', 0, 0)  202 us
    all_gather x1, waiting for transfers between devices, shards(): shard_rows = lax.all_gather(grad_x_b, 'dap', axis=0, tiled=True)  198 us
    psum x1, waiting for transfers between devices, together(): subtotal = lax.psum(jnp.concatenate([a.ravel() for a in arrays]), axis)  150 us
    all_to_all x1, blocking collectives, shards(): lax.all_to_all(left_ib, 'dap', split_axis=1, concat_axis=0, tiled=True)  25.5 us
  transfers between devices with their start and end apart: 4, of which 4 were waited for; matrix products, arithmetic and copies ran while one was open for 2% of the time, Pallas kernels for 0%

profile of v1, /device:TPU:8, one launch (start us, length us, event | category | flops | bytes accessed | tf_op | source)
XLA Modules:
  0.0 959.7 jit_solution(17594330987696849800)
XLA Ops:
  11.6 2.3 multiply_reduce_fusion.4
  18.7 2.8 fusion.12
  21.5 204.8 %all-gather.3.cloned.1.call-done = bf16[192,192,128]{2,1,0:T(8,128)(2,1)} async-done(((bf16[12,192,128]{2,1,0:T(8,128)(2,1)}), bf16[192,192,128]{2,1,0:T(8,128)(2,1)}) %all-gather.3.cloned.1.call-update) | async-done | bytes 9437200 | tf_op jit(solution)/shard_map/all_gather | solution.py:74
  226.2 17.4 %copy.46 = bf16[192,192,128]{1,0,2:T(8,128)(2,1)} copy(bf16[192,192,128]{2,1,0:T(8,128)(2,1)} %all-gather.3.cloned.1.call-done) | data formatting | bytes 18874368 | tf_op jit(solution)/shard_map/all_gather | solution.py:74
  243.6 8.2 bitcast_reduce_fusion
  259.6 25.5 %all_to_all.23 = bf16[12,192,128]{2,0,1:T(8,128)(2,1)S(1)} all-to-all(bf16[12,192,128]{2,0,1:T(8,128)(2,1)S(1)} %copy.49), channel_id=1, replica_groups=mesh['dap'=16,'cplx'=16] {'dap'}, dimensions={1} | all-to-all | bytes 1179648 | tf_op jit(solution)/shard_map/all_to_all | solution.py:91
  285.1 6.0 stack.2
  291.1 4.9 all-to-all-start
  302.0 202.1 %all-to-all-done = bf16[16,12,192,128]{3,2,1,0:T(8,128)(2,1)} async-done(((bf16[16,12,192,128]{3,2,1,0:T(8,128)(2,1)}), bf16[16,12,192,128]{3,2,1,0:T(8,128)(2,1)}, u32[]{:S(2)}, u32[]{:S(2)}) %all-to-all-start) | async-done | bytes 9437216 | tf_op jit(solution)/shard_map/all_to_all | solution.py:97
  504.1 17.4 %copy.52 = bf16[192,192,128]{1,0,2:T(8,128)(2,1)} copy(bf16[192,192,128]{2,1,0:T(8,128)(2,1)} %bitcast.9) | data formatting | bytes 18874368 | tf_op jit(solution)/shard_map/reshape | solution.py:96
  521.5 7.7 fusion.82
  535.5 2.3 add_convert_fusion.1
  538.1 2.6 copy.59
  540.7 2.6 copy.56
  543.4 2.8 fusion.15
  546.1 198.1 %all-gather.5.cloned.1.call-done = bf16[192,192,128]{2,1,0:T(8,128)(2,1)} async-done(((bf16[12,192,128]{2,1,0:T(8,128)(2,1)}), bf16[192,192,128]{2,1,0:T(8,128)(2,1)}) %all-gather.5.cloned.1.call-update) | async-done | bytes 9437200 | tf_op jit(solution)/shard_map/all_gather | solution.py:116
  744.2 17.4 %copy.55 = bf16[192,192,128]{1,0,2:T(8,128)(2,1)} copy(bf16[192,192,128]{2,1,0:T(8,128)(2,1)} %all-gather.5.cloned.1.call-done) | data formatting | bytes 18874368 | tf_op jit(solution)/shard_map/all_gather | solution.py:116
  761.6 9.5 fusion.84
  771.1 2.7 copy.60
  773.8 7.9 fusion.83
  781.7 2.7 copy.57
  784.4 3.7 bitcast_multiply_fusion.3
  796.3 2.5 fusion.22
  798.8 150.0 %all-reduce.6.cloned.1.call-done = bf16[98560]{0:T(1024)(128)(2,1)} async-done(((bf16[98560]{0:T(1024)(128)(2,1)}), bf16[98560]{0:T(1024)(128)(2,1)}) %all-reduce.6.cloned.1.call-update) | async-done | bytes 197136 | tf_op jit(solution)/shard_map/psum | solution.py:11
  (99 shorter events, 41.8 us)
Async XLA Ops:
  7.2 249.0 %copy-start = (bf16[128,512]{1,0:T(8,128)(2,1)S(1)}, bf16[128,512]{1,0:T(8,128)(2,1)}, u32[]{:S(2)}) copy-start(bf16[128,512]{1,0:T(8,128)(2,1)} %param.26) | copy-start | bytes 393220
  7.2 6.9 copy-start.5
  7.2 6.7 copy-start.17
  7.2 6.8 copy-start.19
  7.2 6.8 copy-start.12
  7.2 219.0 %all-gather.3.cloned.1.call-start = ((), (), s32[]{:S(2)}) async-start(), calls=%async_computation.2 | async-start | bytes 10027008 | tf_op jit(solution)/shard_map/all_gather | solution.py:74
  16.7 2.0 copy-start.20
  251.8 0.7 copy-start.18
  252.5 1.3 copy-start.9
  252.5 1.3 copy-start.13
  253.7 2.5 copy-start.16
  257.0 2.2 copy-start.1
  259.2 25.9 %copy-start.7 = (bf16[12,192,128]{2,1,0:T(8,128)(2,1)}, bf16[12,192,128]{2,1,0:T(8,128)(2,1)S(1)}, u32[]{:S(2)}) copy-start(bf16[12,192,128]{2,1,0:T(8,128)(2,1)S(1)} %get-tuple-element.18) | copy-start | bytes 1769476
  259.2 25.9 %copy-start.6 = (bf16[12,192,128]{2,1,0:T(8,128)(2,1)}, bf16[12,192,128]{2,1,0:T(8,128)(2,1)S(1)}, u32[]{:S(2)}) copy-start(bf16[12,192,128]{2,1,0:T(8,128)(2,1)S(1)} %get-tuple-element.19) | copy-start | bytes 1769476
  291.1 5.2 copy-start.14
  291.1 213.0 %all-to-all-start = ((bf16[16,12,192,128]{3,2,1,0:T(8,128)(2,1)}), bf16[16,12,192,128]{3,2,1,0:T(8,128)(2,1)}, u32[]{:S(2)}, u32[]{:S(2)}) async-start(bf16[16,12,192,128]{3,2,1,0:T(8,128)(2,1)} %stack.2), calls=%async_computation | async-start | bytes 18874368 | tf_op jit(solution)/shard_map/all_to_all | solution.py:97
  296.0 448.2 %all-gather.5.cloned.1.call-start = ((), (), s32[]{:S(2)}) async-start(), calls=%async_computation.3 | async-start | bytes 10027008 | tf_op jit(solution)/shard_map/all_gather | solution.py:116
  531.4 1.1 copy-start.2
  531.4 1.1 copy-start.11
  531.4 1.0 copy-start.15
  537.8 411.0 %all-reduce.6.cloned.1.call-start = ((), (), s32[]{:S(2)}) async-start(), calls=%async_computation.4 | async-start | bytes 397312 | tf_op jit(solution)/shard_map/psum | solution.py:11
  789.4 1.1 copy-start.8
  790.2 1.3 copy-start.3
  793.4 2.9 copy-start.4
  (1 other events, 0.7 us)
Sparse Core Ops, SparseCore 0:
  16.8 209.3 all-gather.2
  537.9 206.2 all-gather.4
  796.4 152.3 all-reduce.5
